TPU v7x, 32 devices: a whole 2x2x4 slice. The times are simulated.
32 devices in a mesh: dp: 16 (over z, x, core), head: 2 (over y).
Axes of the slice: x: 2, y: 2, z: 4, core: 2. Of those that a mesh axis runs over, the one named last changes fastest.
Arguments:
- layer_input: bfloat16 [16384, 768], P('dp', 'head'), may hold values from -6 to 6
- first_gain: float32 [768], replicated, may hold values from 0.5 to 1.5
- first_shift: float32 [768], replicated, may hold values from -3 to 3
- qkv_weight: bfloat16 [3, 768, 768], P(None, None, 'head'), may hold values from -0.5 to 0.5
- out_weight: bfloat16 [768, 768], P('head'), may hold values from -0.875 to 0.875
- second_gain: float32 [768], replicated, may hold values from 0.5 to 1.5
- second_shift: float32 [768], replicated, may hold values from -3 to 3
- up_weight: bfloat16 [768, 3072], P(None, 'head'), may hold values from -0.21875 to 0.21875
- down_weight: bfloat16 [3072, 768], P('head'), may hold values from -0.15625 to 0.15625
- segment_ids: int32 [16384], P('dp'), may hold values from 0 to 4, as said below
- pad_mask: int32 [16384], P('dp'), may hold values from 0 to 1, as said below
- cluster_ids: int32 [12, 16384], P('head', 'dp'), may hold values from 0 to 99, as said below
- output_grad: bfloat16 [16384, 768], P('dp', 'head'), may hold values from -6 to 6
Outputs:
- layer_output: bfloat16 [16384, 768], P('dp', 'head')
- input_grad: bfloat16 [16384, 768], P('dp', 'head')
- qkv_grad: float32 [3, 768, 768], P(None, None, 'head')
- mix_weight_grad: float32 [768, 768], P('head')
- up_grad: float32 [768, 3072], P(None, 'head')
- down_grad: float32 [3072, 768], P('head')
- first_gain_grad: float32 [768], replicated
- first_shift_grad: float32 [768], replicated
- second_gain_grad: float32 [768], replicated
- second_shift_grad: float32 [768], replicated
Inputs may be any that keep to these rules, and one draw needn't show every extreme that they name: `segment_ids`: never falling within a sequence of 1024 tokens; 4 documents numbered 0 .. 3, each of 128 tokens or more, then one or more padding tokens numbered 4 at the sequence's end. `pad_mask`: 1 exactly on the tokens of documents, 0 on padding. `cluster_ids`: in each head and sequence every cluster holds at least one token with pad_mask 1, and all such tokens of a cluster lie in one document.
All inputs are finite; a program needn't handle non-finite values.
Results may differ from a plain program's by a relative error of at most 0.015.
The roundings to bfloat16 on the way count: a program that leaves them out, or rounds other values in their place, can miss the bound.
Values may be sent and summed in bfloat16 or wider, within the bound.
A program may use at most 128 MiB of HBM per device.

v0:
```python
import jax
import jax.numpy as jnp
from jax import lax
from jax.sharding import PartitionSpec as P

HDIM = 64
CLUST = 100


epsilon = 1e-05
far_below = -1e30
highest = lax.Precision.HIGHEST


def norm_parts(values):
    row_mean = jnp.mean(values, axis=-1, keepdims=True)
    centred = values - row_mean
    variance = jnp.mean(centred * centred, axis=-1, keepdims=True)
    row_scale = lax.rsqrt(variance + epsilon)
    return (centred * row_scale, row_scale)


def norm_back(upstream, normal, row_scale):
    first_term = jnp.mean(upstream, axis=-1, keepdims=True)
    second_term = jnp.mean(upstream * normal, axis=-1, keepdims=True)
    return row_scale * (upstream - first_term - normal * second_term)


def attention_parts(query, keys, segment_ids, pad_mask, cluster_ids):
    live_rows = (pad_mask > 0).astype(jnp.float32)
    labels = jnp.arange(CLUST, dtype=jnp.int32)
    member = (cluster_ids[:, None, :] == labels[None, :, None]).astype(jnp.float32) * live_rows[
        None, None, :
    ]
    counts = jnp.sum(member, axis=-1)
    member_low = member.astype(jnp.bfloat16)
    centre = (
        jnp.einsum("hcs,she->hce", member_low, query, preferred_element_type=jnp.float32)
        / counts[:, :, None]
    ).astype(jnp.bfloat16)
    seg_float = segment_ids.astype(jnp.float32)
    doc_owner = jnp.einsum("hcs,s->hc", member, seg_float, precision=highest) / counts
    allowed = (jnp.abs(doc_owner[:, :, None] - seg_float[None, None, :]) < 0.5) & (
        pad_mask[None, None, :] > 0
    )
    scores = jnp.einsum(
        "hce,she->hcs", centre, keys, preferred_element_type=jnp.float32
    ) * HDIM ** (-0.5)
    masked = jnp.where(allowed, scores, far_below)
    return (member, member_low, counts, centre, masked)


def shards(
    layer_input,
    first_gain,
    first_shift,
    qkv_weight,
    out_weight,
    second_gain,
    second_shift,
    up_weight,
    down_weight,
    segment_ids,
    pad_mask,
    cluster_ids,
    output_grad,
):
    tokens, local_width = layer_input.shape
    head_count = cluster_ids.shape[0]
    score_scale = HDIM ** (-0.5)
    start = lax.axis_index("head") * local_width
    whole_in = lax.all_gather(layer_input, "head", axis=1, tiled=True).astype(jnp.float32)
    first_hat, first_scale = norm_parts(whole_in)
    normed = (first_hat * first_gain + first_shift).astype(jnp.bfloat16)
    projected = jnp.einsum(
        "td,ide->ite", normed, qkv_weight, preferred_element_type=jnp.float32
    ).astype(jnp.bfloat16)
    head_parts = projected.reshape(3, tokens, head_count, HDIM)
    query, keys, values = (head_parts[0], head_parts[1], head_parts[2])
    member, member_low, counts, centre, masked = attention_parts(
        query, keys, segment_ids, pad_mask, cluster_ids
    )
    row_top = jnp.max(masked, axis=-1, keepdims=True)
    log_total = row_top + jnp.log(jnp.sum(jnp.exp(masked - row_top), axis=-1, keepdims=True))
    weights = jnp.exp(masked - log_total).astype(jnp.bfloat16)
    centre_out = jnp.einsum(
        "hcs,she->hce", weights, values, preferred_element_type=jnp.float32
    ).astype(jnp.bfloat16)
    mixture = (
        jnp.einsum("hcs,hce->she", member_low, centre_out, preferred_element_type=jnp.float32)
        .astype(jnp.bfloat16)
        .reshape(tokens, local_width)
    )
    branch_part = jnp.dot(mixture, out_weight, preferred_element_type=jnp.float32)
    branch = lax.psum_scatter(
        branch_part.astype(jnp.bfloat16), "head", scatter_dimension=1, tiled=True
    ).astype(jnp.float32)
    residual = layer_input.astype(jnp.float32) + branch
    whole_res = lax.all_gather(residual.astype(jnp.bfloat16), "head", axis=1, tiled=True).astype(
        residual.dtype
    )
    second_hat, second_scale = norm_parts(whole_res)
    second = (second_hat * second_gain + second_shift).astype(jnp.bfloat16)
    hidden = jnp.dot(second, up_weight, preferred_element_type=jnp.float32)
    activated, gelu_back = jax.vjp(jax.nn.gelu, hidden)
    activated = activated.astype(jnp.bfloat16)
    ffn_part = jnp.dot(activated, down_weight, preferred_element_type=jnp.float32)
    ffn_out = lax.psum_scatter(
        ffn_part.astype(jnp.bfloat16), "head", scatter_dimension=1, tiled=True
    ).astype(jnp.float32)
    layer_output = (residual + ffn_out).astype(jnp.bfloat16)
    whole_grad = lax.all_gather(output_grad, "head", axis=1, tiled=True)
    down_grad = jnp.einsum("tf,td->fd", activated, whole_grad, preferred_element_type=jnp.float32)
    act_grad = jnp.einsum("td,fd->tf", whole_grad, down_weight, preferred_element_type=jnp.float32)
    hidden_grad = gelu_back(act_grad)[0].astype(jnp.bfloat16)
    up_grad = jnp.einsum("td,tf->df", second, hidden_grad, preferred_element_type=jnp.float32)
    second_part = jnp.einsum(
        "tf,df->td", hidden_grad, up_weight, preferred_element_type=jnp.float32
    )
    second_back = lax.psum(second_part, "head")
    second_gain_grad = jnp.sum(second_back * second_hat, axis=0)
    second_shift_grad = jnp.sum(second_back, axis=0)
    residual_grad = whole_grad.astype(jnp.float32) + norm_back(
        second_back * second_gain, second_hat, second_scale
    )
    branch_grad = residual_grad.astype(jnp.bfloat16)
    mix_weight_grad = jnp.einsum(
        "te,td->ed", mixture, branch_grad, preferred_element_type=jnp.float32
    )
    mixture_grad = jnp.einsum(
        "td,ed->te", branch_grad, out_weight, preferred_element_type=jnp.float32
    ).reshape(tokens, head_count, HDIM)
    centre_out_grad = jnp.einsum("hcs,she->hce", member, mixture_grad, precision=highest).astype(
        jnp.bfloat16
    )
    probs = jnp.exp(masked - log_total)
    prob_grad = jnp.einsum(
        "hce,she->hcs", centre_out_grad, values, preferred_element_type=jnp.float32
    )
    value_grad = jnp.einsum(
        "hcs,hce->she", weights, centre_out_grad, preferred_element_type=jnp.float32
    )
    score_grad = (probs * (prob_grad - jnp.sum(prob_grad * probs, axis=-1, keepdims=True))).astype(
        jnp.bfloat16
    )
    centre_grad = (
        jnp.einsum("hcs,she->hce", score_grad, keys, preferred_element_type=jnp.float32)
        * score_scale
    )
    key_grad = (
        jnp.einsum("hcs,hce->she", score_grad, centre, preferred_element_type=jnp.float32)
        * score_scale
    )
    query_grad = jnp.einsum(
        "hcs,hce->she", member, centre_grad / counts[:, :, None], precision=highest
    )
    proj_grad = (
        jnp.stack([query_grad, key_grad, value_grad])
        .reshape(3, tokens, local_width)
        .astype(jnp.bfloat16)
    )
    qkv_grad = jnp.einsum("td,ite->ide", normed, proj_grad, preferred_element_type=jnp.float32)
    first_part = jnp.einsum(
        "ite,ide->td", proj_grad, qkv_weight, preferred_element_type=jnp.float32
    )
    first_back = lax.psum(first_part.astype(jnp.bfloat16), "head").astype(jnp.float32)
    first_gain_grad = jnp.sum(first_back * first_hat, axis=0)
    first_shift_grad = jnp.sum(first_back, axis=0)
    input_full = residual_grad + norm_back(first_back * first_gain, first_hat, first_scale)
    input_grad = lax.dynamic_slice_in_dim(input_full, start, local_width, 1).astype(jnp.bfloat16)
    summed = lax.psum(
        (
            qkv_grad,
            mix_weight_grad,
            up_grad,
            down_grad,
            first_gain_grad,
            first_shift_grad,
            second_gain_grad,
            second_shift_grad,
        ),
        "dp",
    )
    (
        qkv_total,
        mix_total,
        up_total,
        down_total,
        first_gain_total,
        first_shift_total,
        second_gain_total,
        second_shift_total,
    ) = summed
    return (
        layer_output,
        input_grad,
        qkv_total,
        mix_total,
        up_total,
        down_total,
        first_gain_total,
        first_shift_total,
        second_gain_total,
        second_shift_total,
    )


def solution(mesh):
    placed = (
        P("dp", "head"),
        P(),
        P(),
        P(None, None, "head"),
        P("head", None),
        P(),
        P(),
        P(None, "head"),
        P("head", None),
        P("dp"),
        P("dp"),
        P("head", "dp"),
        P("dp", "head"),
    )
    return jax.shard_map(
        shards,
        mesh=mesh,
        in_specs=placed,
        out_specs=(
            P("dp", "head"),
            P("dp", "head"),
            P(None, None, "head"),
            P("head", None),
            P(None, "head"),
            P("head", None),
            P(),
            P(),
            P(),
            P(),
        ),
        check_vma=False,
    )
```

profile of v0, /device:TPU:0, one launch (start us, length us, event | category | flops | bytes accessed | tf_op | source)
XLA Modules:
  0.0 614.3 jit_solution(7935351262349309971)
XLA Ops:
  7.2 0.7 all-gather.4.cloned.1.call-update
  8.0 0.7 convert_element_type.94
  8.7 0.7 fusion.89
  9.4 1.1 select_reduce_fusion
  10.5 3.3 fusion.11
  13.8 25.7 %all-gather.4.cloned.1.call-done = bf16[1024,768]{1,0:T(8,128)(2,1)} async-done(((bf16[1024,384]{1,0:T(8,128)(2,1)}), bf16[1024,768]{1,0:T(8,128)(2,1)}) %all-gather.4.cloned.1.call-update) | async-done | bytes 1572880 | tf_op jit(solution)/shard_map/all_gather | solution.py:72
  39.5 1.8 convert_reduce_fusion.2
  41.4 0.6 fusion.29
  42.0 3.8 convert_bitcast_fusion
  46.1 0.5 copy-done.25
  46.6 0.6 fusion.62
  47.2 1.2 fusion.91
  48.4 1.5 copy-done.2
  49.8 0.7 exponential_reduce_fusion
  50.5 3.8 fusion.40
  54.3 3.5 convolution_convert_fusion
  57.8 2.6 copy.38
  60.4 0.7 all-gather.8.cloned.1.call-update
  61.1 25.5 %reduce-scatter.7.cloned.1.call-done = bf16[384,1024]{1,0:T(8,128)(2,1)} async-done(((bf16[768,1024]{1,0:T(8,128)(2,1)}), bf16[384,1024]{1,0:T(8,128)(2,1)}) %reduce-scatter.7.cloned.1.call-update) | async-done | bytes 786448
  86.7 2.3 copy.39
  89.0 2.2 fusion.39
  91.4 24.0 %all-gather.8.cloned.1.call-done = bf16[1024,768]{1,0:T(8,128)(2,1)} async-done(((bf16[1024,384]{1,0:T(8,128)(2,1)}), bf16[1024,768]{1,0:T(8,128)(2,1)}) %all-gather.8.cloned.1.call-update) | async-done | bytes 1572880 | tf_op jit(solution)/shard_map/all_gather | solution.py:112
  115.4 7.4 %fusion.92 = f32[1024,1536]{1,0:T(8,128)} fusion(bf16[1024,768]{1,0:T(8,128)(2,1)} %all-gather.8.cloned.1.call-done, bf16[1536,768]{1,0:T(8,128)(2,1)} %param.21), kind=kOutput, calls=%fused_computation.127 | convolution fusion | flops 2415919104 | bytes 10223616 | tf_op jit(solution)/shard_map/td,fd->tf/dot_general | solution.py:114
  122.9 21.8 %all-gather.6.cloned.1.call-done = bf16[1024,768]{1,0:T(8,128)(2,1)} async-done(((bf16[1024,384]{1,0:T(8,128)(2,1)}), bf16[1024,768]{1,0:T(8,128)(2,1)}) %all-gather.6.cloned.1.call-update) | async-done | bytes 1572880 | tf_op jit(solution)/shard_map/all_gather | solution.py:99
  144.6 1.8 convert_reduce_fusion.1
  146.5 0.6 fusion.28
  147.2 9.7 %fusion.6 = (bf16[1024,1536]{1,0:T(8,128)(2,1)S(1)}, f32[1024,1536]{1,0:T(8,128)}) fusion(f32[1024,1536]{1,0:T(8,128)} %fusion.92, bf16[768,1536]{1,0:T(8,128)(2,1)S(1)} %copy-done, bf16[1024,768]{1,0:T(8,128)(2,1)S(1)} %copy-done.7, f32[768]{0:T(1024)S(1)} %copy-done.28, f32[768]{0:T(1024)S(1)} %copy-done.26, f32[1024]{0:T(1024)S(1)} %add_rsqrt_fusion, ...), kind=kOutput, calls=%fused_computation.8 | convolution fusion | flops 2452094976 | bytes 19675136 | tf_op jit(solution)/shard_map/dot_general | solution.py:104
  156.9 1.7 copy-done.30
  158.6 4.3 fusion.93
  163.0 7.2 %convolution_convert_fusion.1 = bf16[1024,768]{1,0:T(8,128)(2,1)S(1)} fusion(bf16[1536,768]{1,0:T(8,128)(2,1)} %param.21, f32[1024,1536]{1,0:T(8,128)} %get-tuple-element.56), kind=kOutput, calls=%fused_computation.60 | convolution fusion | flops 2430861312 | bytes 10223616 | tf_op jit(solution)/shard_map/dot_general | solution.py:107
  170.2 1.6 copy.40
  171.9 9.2 %fusion.86 = f32[1536,768]{1,0:T(8,128)} fusion(bf16[1024,768]{1,0:T(8,128)(2,1)} %all-gather.8.cloned.1.call-done, f32[1024,1536]{1,0:T(8,128)} %get-tuple-element.56), kind=kOutput, calls=%fused_computation.123 | convolution fusion | flops 2430074880 | bytes 12582912 | tf_op jit(solution)/shard_map/tf,td->fd/dot_general | solution.py:113
  181.1 67.8 %all-reduce.6.cloned.1.call-done = f32[1024,768]{1,0:T(8,128)} async-done(((f32[1024,768]{1,0:T(8,128)}), f32[1024,768]{1,0:T(8,128)}) %all-reduce.6.cloned.1.call-update) | async-done | bytes 3145744 | tf_op jit(solution)/shard_map/psum | solution.py:120
  248.9 3.4 fusion.27
  252.4 1.4 fusion.26
  253.8 0.8 fusion.68
  254.6 0.8 copy-done.5
  255.4 3.2 fusion.63
  258.7 0.7 convolution_convert_fusion.2
  259.4 1.2 copy.32
  260.6 2.8 multiply_reduce_fusion.2
  263.5 0.5 multiply_convert_fusion.1
  264.0 1.0 copy-done.14
  265.1 0.4 multiply_convert_fusion.2
  265.5 1.1 copy.31
  266.6 2.2 fusion.61
  268.8 2.7 fusion.41
  271.5 2.3 copy.30
  273.8 5.3 bitcast_convert_fusion
  279.2 6.9 %fusion.82 = f32[768,1536]{1,0:T(8,128)} fusion(bf16[1024,1536]{1,0:T(8,128)(2,1)} %copy-done.30, bf16[1024,768]{1,0:T(8,128)(2,1)S(1)} %copy-done.8, f32[768]{0:T(1024)S(1)} %copy-done.28, f32[768]{0:T(1024)S(1)} %copy-done.26, f32[1024]{0:T(1024)S(1)} %add_rsqrt_fusion, f32[1024]{0:T(1024)S(1)} %broadcast_multiply_fusion.4), kind=kOutput, calls=%fused_computation.121 | convolution fusion | flops 2420637696 | bytes 9451520 | tf_op jit(solution)/shard_map/td,tf->df/dot_general | solution.py:116
  286.2 1.8 fusion.66
  288.1 0.5 copy-done.23
  288.6 4.3 convolution_bitcast_fusion
  293.0 2.3 copy.41
  295.3 2.3 add_convert_fusion.1
  297.6 33.4 %all-reduce.8.cloned.1.call-done = bf16[1024,768]{1,0:T(8,128)(2,1)} async-done(((bf16[1024,768]{1,0:T(8,128)(2,1)}), bf16[1024,768]{1,0:T(8,128)(2,1)}) %all-reduce.8.cloned.1.call-update) | async-done | bytes 1572880 | tf_op jit(solution)/shard_map/psum | solution.py:166
  331.0 4.6 fusion.30
  335.6 64.1 %all-reduce = (f32[768]{0:T(1024)}, f32[768]{0:T(1024)}, f32[768]{0:T(1024)}, f32[768]{0:T(1024)}) all-reduce(f32[768]{0:T(1024)S(1)} %get-tuple-element.32, f32[768]{0:T(1024)S(1)} %get-tuple-element.37, f32[768]{0:T(1024)S(1)} %get-tuple-element.30, f32[768]{0:T(1024)S(1)} %get-tuple-element.35), channel_id=1, replica_groups=mesh['dp'=16,'head'=2] {'dp'}, use_global_device_ids=true, to_apply=%region_21.22 | all-reduce | flops 3072 | bytes 24576 | tf_op jit(solution)/shard_map/psum | solution.py:171
  399.7 3.8 fusion.36
  403.4 189.6 %all-reduce.10.cloned.1.call-done = (f32[3,768,384]{1,2,0:T(8,128)}, f32[384,768]{1,0:T(8,128)}, f32[768,1536]{1,0:T(8,128)}, f32[1536,768]{1,0:T(8,128)}) async-done(((f32[3,768,384]{1,2,0:T(8,128)}, f32[384,768]{1,0:T(8,128)}, f32[768,1536]{1,0:T(8,128)}, f32[1536,768]{1,0:T(8,128)}), (f32[3,768,384]{1,2,0:T(8,128)}, f32[384,768]{1,0:T(8,128)}, f32[768,1536]{1,0:T(8,128)}, ...) | async-done | bytes 14155792 | tf_op jit(solution)/shard_map/psum | solution.py:171
  593.0 5.2 copy.34
  598.3 1.0 copy.49
  599.3 5.5 copy.50
  604.8 2.2 copy.51
  (86 shorter events, 1.3 us)
Async XLA Ops:
  7.2 140.0 %copy-start = (bf16[768,1536]{1,0:T(8,128)(2,1)S(1)}, bf16[768,1536]{1,0:T(8,128)(2,1)}, u32[]{:S(2)}) copy-start(bf16[768,1536]{1,0:T(8,128)(2,1)} %param.20) | copy-start | bytes 7077892
  7.2 32.3 %all-gather.4.cloned.1.call-start = ((), (), s32[]{:S(2)}) async-start(), calls=%async_computation.2 | async-start | bytes 2359296 | tf_op jit(solution)/shard_map/all_gather | solution.py:72
  7.9 34.1 %copy-start.27 = (f32[768]{0:T(1024)S(1)}, f32[768]{0:T(1024)}, u32[]{:S(2)}) copy-start(f32[768]{0:T(1024)} %param.14) | copy-start | bytes 9220
  7.9 34.1 %copy-start.29 = (f32[768]{0:T(1024)S(1)}, f32[768]{0:T(1024)}, u32[]{:S(2)}) copy-start(f32[768]{0:T(1024)} %param.15) | copy-start | bytes 9220
  7.9 78.7 %reduce-scatter.7.cloned.1.call-start = ((), (), s32[]{:S(2)}) async-start(), calls=%async_computation.7 | async-start | bytes 2359296
  39.5 1.9 copy-start.9
  45.8 0.8 copy-start.25
  46.1 2.3 copy-start.19
  46.1 4.4 copy-start.15
  48.3 1.5 copy-start.2
  60.3 28.6 %copy-start.12 = (bf16[1024,384]{1,0:T(8,128)(2,1)S(1)}, bf16[1024,384]{1,0:T(8,128)(2,1)}, u32[]{:S(2)}) copy-start(bf16[1024,384]{1,0:T(8,128)(2,1)} %param.13) | copy-start | bytes 2359300
  60.4 55.1 %all-gather.8.cloned.1.call-start = ((), (), s32[]{:S(2)}) async-start(), calls=%async_computation.4 | async-start | bytes 2359296 | tf_op jit(solution)/shard_map/all_gather | solution.py:112
  61.1 83.5 %all-gather.6.cloned.1.call-start = ((), (), s32[]{:S(2)}) async-start(), calls=%async_computation.3 | async-start | bytes 2359296 | tf_op jit(solution)/shard_map/all_gather | solution.py:99
  91.2 157.7 %all-reduce.6.cloned.1.call-start = ((), (), s32[]{:S(2)}) async-start(), calls=%async_computation.5 | async-start | bytes 6291456 | tf_op jit(solution)/shard_map/psum | solution.py:120
  122.9 24.3 %copy-start.26 = (f32[768]{0:T(1024)S(1)}, f32[768]{0:T(1024)}, u32[]{:S(2)}) copy-start(f32[768]{0:T(1024)} %param.18) | copy-start | bytes 9220
  122.9 24.3 %copy-start.28 = (f32[768]{0:T(1024)S(1)}, f32[768]{0:T(1024)}, u32[]{:S(2)}) copy-start(f32[768]{0:T(1024)} %param.19) | copy-start | bytes 9220
  144.6 1.9 copy-start.7
  156.9 1.7 copy-start.30
  162.9 130.0 %reduce-scatter.9.cloned.1.call-start = ((), (), s32[]{:S(2)}) async-start(), calls=%async_computation.8 | async-start | bytes 2359296
  171.9 77.0 %copy-start.8 = (bf16[1024,768]{1,0:T(8,128)(2,1)S(1)}, bf16[1024,768]{1,0:T(8,128)(2,1)}, u32[]{:S(2)}) copy-start(bf16[1024,768]{1,0:T(8,128)(2,1)} %all-gather.6.cloned.1.call-done) | copy-start | bytes 4718596
  171.9 159.1 %all-reduce.8.cloned.1.call-start = ((), (), s32[]{:S(2)}) async-start(), calls=%async_computation.6 | async-start | bytes 3145728 | tf_op jit(solution)/shard_map/psum | solution.py:166
  248.9 3.4 copy-start.11
  248.9 3.4 copy-start.16
  252.4 1.4 copy-start.24
  253.8 1.6 copy-start.5
  255.4 3.3 copy-start.3
  260.6 2.8 copy-start.4
  264.0 1.0 copy-start.14
  266.6 7.2 %copy-start.20 = (bf16[1,1024,384]{2,1,0:T(8,128)(2,1)S(1)}, bf16[1,1024,384]{2,1,0:T(8,128)(2,1)}, u32[]{:S(2)}) copy-start(bf16[1,1024,384]{2,1,0:T(8,128)(2,1)} %copy.32) | copy-start | bytes 2359300
  279.2 6.9 %copy-start.18 = (bf16[6,64,1024]{2,1,0:T(8,128)(2,1)S(1)}, bf16[6,64,1024]{2,1,0:T(8,128)(2,1)}, u32[]{:S(2)}) copy-start(bf16[6,64,1024]{2,1,0:T(8,128)(2,1)} %fusion.40) | copy-start | bytes 2359300
  279.2 313.8 %all-reduce.10.cloned.1.call-start = ((), (), s32[]{:S(2)}) async-start(), calls=%async_computation.9 | async-start | bytes 28311552 | tf_op jit(solution)/shard_map/psum | solution.py:171
  279.2 6.9 %copy-start.6 = (f32[1024,768]{1,0:T(8,128)S(1)}, f32[1024,768]{1,0:T(8,128)}, u32[]{:S(2)}) copy-start(f32[1024,768]{1,0:T(8,128)} %copy-done.5) | copy-start | bytes 9437188
  286.1 1.9 copy-start.10
  286.1 1.9 copy-start.21
  286.1 2.0 copy-start.22
  286.1 2.5 copy-start.23
  292.9 2.4 copy-start.13
  593.0 5.3 copy-start.17
  598.3 6.5 %slice-start = ((s8[4718592]{0:T(1024)(128)(4,1)}), s8[4194304]{0:T(1024)(128)(4,1)S(1)}, s32[]{:S(2)}) async-start(s8[4718592]{0:T(1024)(128)(4,1)} %bitcast.63), calls=%async_computation.10 | async-start | bytes 8388608
  599.3 5.5 slice-start.1
  599.3 7.7 %copy-start.1 = (bf16[768,1536]{1,0:T(8,128)(2,1)S(1)}, bf16[768,1536]{1,0:T(8,128)(2,1)}, u32[]{:S(2)}) copy-start(bf16[768,1536]{1,0:T(8,128)(2,1)} %param.20) | copy-start | bytes 7077892
Sparse Core Ops, SparseCore 0:
  9.5 29.9 all-gather.3
  60.5 26.1 reduce-scatter.6
  88.2 27.1 all-gather.7
  117.4 27.1 all-gather.5
  163.0 85.8 all-reduce.5
  251.0 26.1 reduce-scatter.8
  279.5 51.5 all-reduce.7
  336.2 256.7 all-reduce.9
where the time goes:
time: 623 us; the launch traced here: 614 us
  waiting for transfers between devices  389 us (62%)
  matrix products  85.2 us (14%)
  blocking collectives  64.1 us (10%)
  local copies, waits for them, and re-layouts  34.1 us (5%)
  other arithmetic  26.2 us (4%)
  between operations  15 us (2%)
    psum x1, waiting for transfers between devices, shards(): lax.psum((qkv_grad, mix_weight_grad, up_grad, down_grad, first_gain_grad,...  190 us
    psum x1, waiting for transfers between devices, shards(): second_back = lax.psum(second_part, 'head')  67.8 us
    psum x1, blocking collectives, shards(): lax.psum((qkv_grad, mix_weight_grad, up_grad, down_grad, first_gain_grad,...  64.1 us
    psum x1, waiting for transfers between devices, shards(): lax.psum(first_part.astype(jnp.bfloat16), 'head').astype(jnp.float32)  33.4 us
    unnamed x74, local copies, waits for them, and re-layouts  29.2 us
    unnamed x10, waiting for transfers between devices  27 us
    all_gather x1, waiting for transfers between devices, shards(): lax.all_gather(layer_input, 'head', axis=1, tiled=True).astype(jnp.float32)  25.7 us
    all_gather x1, waiting for transfers between devices, shards(): whole_grad = lax.all_gather(output_grad, 'head', axis=1, tiled=True)  24 us
  transfers between devices with their start and end apart: 8, of which 7 were waited for; matrix products, arithmetic and copies ran while one was open for 15% of the time, Pallas kernels for 0%

commit v1 on v0

v1 whole, which is shorter than its diff:
```python
import functools

import jax
import jax.numpy as jnp
from jax import lax
from jax.experimental import pallas as pl
from jax.experimental.pallas import tpu as pltpu
from jax.sharding import PartitionSpec as P

HDIM = 64
CLUST = 100
CPAD = 128
TILE = 256
CHUNK = 512
EPS = 1e-05
FAR = -1e30
SCALE = HDIM**-0.5
C0 = 0.7978845608028654
C1 = 0.044715 * C0
MESH = pl.DeviceIdType.MESH
f32, bf16, i32 = jnp.float32, jnp.bfloat16, jnp.int32


def nn(a, b):
    return lax.dot_general(a, b, (((1,), (0,)), ((), ())), preferred_element_type=f32)


def nt(a, b):
    return lax.dot_general(a, b, (((1,), (1,)), ((), ())), preferred_element_type=f32)


def tn(a, b):
    return lax.dot_general(a, b, (((0,), (0,)), ((), ())), preferred_element_type=f32)


def ds(start, size, unit=None):
    if isinstance(start, int):
        return pl.ds(start, size)
    return pl.ds(pl.multiple_of(start, size if unit is None else unit), size)


def loop(count, body):
    def step(i, carry):
        body(i)
        return carry

    lax.fori_loop(0, count, step, 0)


def plan(rows, order):
    steps = []
    for step in order:
        halve = (rows // 2) % 16 == 0
        if halve:
            rows //= 2
        steps.append((step, rows, halve))
    return steps


class Total:
    def __init__(self, rt, rows, cols, order, acc, base, sends, recvs, out):
        self.rt, self.cols, self.acc, self.base, self.out = rt, cols, acc, base, out
        self.steps = plan(rows, order)
        self.sends, self.recvs = sends, recvs
        self.copies = []
        self.back = []
        self.at = 0
        self.size = rows
        self.pos = 0

    def bit(self, k):
        return (self.rt.place // self.steps[k][0]) % 2

    def peer(self, k):
        return self.rt.across(self.steps[k][0])

    def send(self, k):
        rows = self.steps[k][1]
        copy = self.rt.remote(self.sends[k], self.recvs[k], self.peer(k))
        copy.start()
        self.copies.append(copy)

    def first_sent(self):
        self.send(0)
        self.size //= 2
        self.at = self.bit(0) * self.size

    def move(self):
        k = self.pos
        self.pos += 1
        n = len(self.steps)
        if k < n:
            self.copies[k].wait()
            rows, halve = self.steps[k][1], self.steps[k][2]
            recv = self.recvs[k]
            acc, base = self.acc, self.base
            unit = 16
            own = None if halve else self.sends[k]
            if k + 1 < n:
                nrows, nhalve = self.steps[k + 1][1], self.steps[k + 1][2]
                out = self.sends[k + 1]
                if nhalve:
                    bit = self.bit(k + 1)
                    away, kept = (1 - bit) * nrows, bit * nrows

                    def cast(i):
                        r = ds(away + i * unit, unit)
                        a = ds(base + away + i * unit, unit)
                        out[ds(i * unit, unit), :] = self.join(acc, a, recv, own, r).astype(bf16)

                    loop(nrows // unit, cast)
                    self.send(k + 1)

                    def add(i):
                        r = ds(kept + i * unit, unit)
                        a = ds(base + kept + i * unit, unit)
                        acc[a, :] = self.join(acc, a, recv, own, r)

                    loop(nrows // unit, add)
                    self.base = base + kept
                    self.at = self.at + kept
                    self.size = nrows
                else:

                    def both(i):
                        r = ds(i * unit, unit)
                        a = ds(base + i * unit, unit)
                        v = self.join(acc, a, recv, own, r)
                        acc[a, :] = v
                        out[r, :] = v.astype(bf16)

                    loop(nrows // unit, both)
                    self.send(k + 1)
            else:

                def last(i):
                    r = ds(i * unit, unit)
                    a = ds(base + i * unit, unit)
                    o = ds(self.at + i * unit, unit)
                    self.out[o, :] = self.join(acc, a, recv, own, r).astype(bf16)

                loop(rows // unit, last)
                self.todo = [j for j in range(n) if self.steps[j][2]]
                self.gather()
            return
        self.back[-1].wait()
        self.gather()

    def join(self, acc, a, recv, own, r):
        mine = acc[a, :] if own is None else own[r, :].astype(f32)
        return mine + recv[r, :].astype(f32)

    def gather(self):
        if self.back:
            j = self.todo.pop()
            self.at = self.at - self.bit(j) * self.steps[j][1]
            self.size *= 2
        if not self.todo:
            return
        j = self.todo[-1]
        rows = self.out.at[ds(self.at, self.size, 16), :]
        copy = self.rt.remote(rows, rows, self.peer(j))
        copy.start()
        self.back.append(copy)

    @property
    def left(self):
        return len(self.steps) + sum(s[2] for s in self.steps) - self.pos


class Runtime:
    def __init__(self, nbits, send_sem, recv_sem, local_sem):
        self.place = lax.axis_index("dp")
        self.hd = lax.axis_index("head")
        self.nbits = nbits
        self.send_sem, self.recv_sem, self.local_sem = send_sem, recv_sem, local_sem
        self.used = self.used_local = 0

    def across(self, step):
        bit = (self.place // step) % 2
        return (self.place + step * (1 - 2 * bit), self.hd)

    @property
    def beside(self):
        return (self.place, 1 - self.hd)

    def take(self, count=1):
        self.used += count
        return self.used - count

    def remote(self, src, dst, peer, sem=None):
        k = self.take() if sem is None else sem
        return pltpu.make_async_remote_copy(
            src_ref=src,
            dst_ref=dst,
            send_sem=self.send_sem.at[k],
            recv_sem=self.recv_sem.at[k],
            device_id=peer,
            device_id_type=MESH,
        )

    def local(self, src, dst, sem=None):
        if sem is None:
            sem = self.used_local
            self.used_local += 1
        return pltpu.make_async_copy(src, dst, self.local_sem.at[sem])

    def enter(self):
        barrier = pltpu.get_barrier_semaphore()
        peers = [self.beside] + [self.across(1 << k) for k in range(self.nbits)]
        for peer in peers:
            pl.semaphore_signal(barrier, inc=1, device_id=peer, device_id_type=MESH)
        pl.semaphore_wait(barrier, len(peers))


def layer_kernel(names, nbits, orders, *refs):
    (x_in, og_in, w_in, ow_in, up_in, dn_in, ids_in, gv_in) = refs[:8]
    (lo_out, ig_out, q_out, m_out, u_out, d_out, g_out) = refs[8:15]
    s = dict(zip(names, refs[15:]))
    T, DL = x_in.shape
    D, FL = up_in.shape
    HL = DL // HDIM
    NP = HL // 2
    tiles = T // TILE
    rt = Runtime(nbits, s["send_sem"], s["recv_sem"], s["local_sem"])
    hd = rt.hd
    core = rt.place % 2
    X, OG, NRM, QKV, W, OW, UP, DN = (s[n] for n in ("X", "OG", "NRM", "QKV", "W", "OW", "UP", "DN"))
    IDS, IDE, IDT, GV, STATS, AUX = (s[n] for n in ("IDS", "IDE", "IDT", "GV", "STATS", "AUX"))
    MIX, RES, SEC, ACT, HG = (s[n] for n in ("MIX", "RES", "SEC", "ACT", "HG"))
    MB, SB, DB, WB, CEN, CO = (s[n] for n in ("MB", "SB", "DB", "WB", "CEN", "CO"))
    SCOL = s["SCOL"]
    HB, AB, PB = SB.at[:, pl.ds(0, CHUNK)], DB.at[:, pl.ds(0, CHUNK)], DB.at[:, pl.ds(0, D)]
    mine = ds(hd * DL, DL, 128)
    away = ds((1 - hd) * DL, DL, 128)

    def x_local(m):
        rows = ds(m * TILE, TILE)
        return rt.local(x_in.at[rows, :], X.at[rows, mine], sem=m)

    def og_local():
        return rt.local(og_in, OG.at[:, mine], sem=tiles)

    for m in range(tiles):
        x_local(m).start()
    rt.used_local = tiles + 1
    cp_ids = rt.local(ids_in, IDS.at[hd])
    cp_ids.start()
    cp_gv = rt.local(gv_in, GV)
    cp_gv.start()
    cp_w = rt.local(w_in, W)
    cp_w.start()
    cp_ow = rt.local(ow_in, OW.at[ds(hd * DL, DL, 16), :])
    cp_ow.start()
    og_local().start()
    cp_up = rt.local(up_in, UP)
    cp_up.start()
    cp_dn = rt.local(dn_in, DN)
    cp_dn.start()

    rt.enter()

    k_x, k_og = rt.take(tiles), rt.take(tiles)

    def x_remote(m):
        rows = ds(m * TILE, TILE)
        return rt.remote(x_in.at[rows, :], X.at[rows, mine], rt.beside, sem=k_x + m)

    def og_remote(m):
        rows = ds(m * TILE, TILE)
        return rt.remote(og_in.at[rows, :], OG.at[rows, mine], rt.beside, sem=k_og + m)

    cp_idr = rt.remote(ids_in, IDS.at[hd], rt.beside)
    cp_idr.start()
    for m in range(tiles):
        x_remote(m).start()
    half = DL // 2
    cp_owr = rt.remote(
        ow_in.at[ds(core * half, half, 16), :],
        OW.at[ds(hd * DL + core * half, half, 16), :],
        rt.beside,
    )
    cp_owr.start()
    og_remote(0).start()
    og_remote(1).start()

    cp_ids.wait()
    cp_idr.wait()
    cp_gv.wait()
    for h in range(2):
        ids = IDS[h]
        keep = ids[7:8, :] > 0
        ide = jnp.where(keep, ids, -1)
        IDE[h] = ide
        IDT[:, h * 8 : h * 8 + 8] = jnp.transpose(ide)
    g1, b1, g2, b2 = (GV[i : i + 1, :] for i in range(4))

    def p1(m):
        x_local(m).wait()
        x_remote(m).wait()
        unit = 32

        def norm(i):
            r = ds(m * TILE + i * unit, unit)
            v = X[r, :].astype(f32)
            mean = jnp.mean(v, axis=1, keepdims=True)
            c = v - mean
            rs = lax.rsqrt(jnp.mean(c * c, axis=1, keepdims=True) + EPS)
            NRM[r, :] = (c * rs * GV[0:1, :] + GV[1:2, :]).astype(bf16)
            STATS[r, 0:1] = mean
            STATS[r, 1:2] = rs

        loop(TILE // unit, norm)
        rows = ds(m * TILE, TILE)
        for i in range(3):
            QKV[i, rows, :] = nn(NRM[rows, :], W[i]).astype(bf16)

    cp_w.wait()
    loop(tiles, p1)

    cp_owr.wait()
    relay = OW.at[ds((1 - hd) * DL + core * half, half, 16), :]
    cp_owc = rt.remote(relay, relay, rt.across(1))
    cp_owc.start()

    low = lax.broadcasted_iota(i32, (CPAD, 128), 1) < HDIM

    def split(v):
        zero = jnp.zeros_like(v)
        return jnp.concatenate([jnp.where(low, v, zero), jnp.where(low, zero, v)], axis=0)

    def fold(v):
        return jnp.where(low, v[:CPAD], v[CPAD:])

    def members(h, p):
        unit = 16
        for a in range(2):
            k = 2 * p + a

            def fill(i):
                row = IDE[h, k : k + 1, :]
                c = lax.broadcasted_iota(i32, (unit, T), 0) + i * unit
                MB[ds(a * CPAD + i * unit, unit), :] = jnp.where(row == c, 1.0, 0.0).astype(bf16)

            loop(CPAD // unit, fill)

    def columns(cols, p):
        lane = lax.broadcasted_iota(i32, (TILE, CPAD), 1)
        parts = []
        for a in range(2):
            k = 2 * p + a
            parts.append(jnp.where(cols[:, k : k + 1] == lane, 1.0, 0.0).astype(bf16))
        return jnp.concatenate(parts, axis=1)

    def own_ids(rows):
        return jnp.where(hd == 0, IDT[rows, 0:8], IDT[rows, 8:16])

    def masked_scores(p, r):
        seg = IDE[hd, 6:7, :].astype(f32)
        allowed = jnp.abs(AUX[p, r, 1:2] - seg) < 0.5
        return jnp.where(allowed, SB[r, :] * SCALE, FAR)

    co_sent = []
    for p in range(NP):
        lanes = pl.ds(p * 128, 128)
        members(hd, p)
        unit = 16

        def count(i):
            r = ds(i * unit, unit)
            v = MB[r, :].astype(f32)
            n = jnp.maximum(jnp.sum(v, axis=1, keepdims=True), 1.0)
            seg = IDE[hd, 6:7, :].astype(f32)
            AUX[p, r, 0:1] = 1.0 / n
            AUX[p, r, 1:2] = jnp.sum(v * seg, axis=1, keepdims=True) / n

        loop(2 * CPAD // unit, count)
        cen = (nn(MB[...], QKV[0, :, lanes]) * AUX[p, :, 0:1]).astype(bf16)
        CEN[p] = split(fold(cen))
        SB[...] = nt(CEN[p], QKV[1, :, lanes])

        def soft(i):
            r = ds(i * unit, unit)
            v = masked_scores(p, r)
            top = jnp.max(v, axis=1, keepdims=True)
            e = jnp.exp(v - top)
            den = jnp.sum(e, axis=1, keepdims=True)
            WB[r, :] = (e * (1.0 / den)).astype(bf16)
            AUX[p, r, 2:3] = top + jnp.log(den)

        loop(2 * CPAD // unit, soft)
        CO[hd * NP + p] = fold(nn(WB[...], QKV[2, :, lanes]).astype(bf16))
        there = CO.at[hd * NP + p]
        copy = rt.remote(there, there, rt.beside)
        copy.start()
        co_sent.append(copy)

    for m in range(2, tiles):
        og_remote(m).start()

    cp_ow.wait()
    cp_owc.wait()
    for copy in co_sent:
        copy.wait()

    def p3(m):
        rows = ds(m * TILE, TILE)
        for q in range(2 * NP):
            h, p = q // NP, q % NP
            MIX[rows, q * 128 : (q + 1) * 128] = nn(columns(IDT[rows, h * 8 : h * 8 + 8], p), split(CO[q])).astype(bf16)
        PB[...] = nn(MIX[rows, :], OW[...])
        unit = 32

        def norm(i):
            r = ds(m * TILE + i * unit, unit)
            v = X[r, :].astype(f32) + PB[ds(i * unit, unit), :]
            RES[r, :] = v
            mean = jnp.mean(v, axis=1, keepdims=True)
            c = v - mean
            rs = lax.rsqrt(jnp.mean(c * c, axis=1, keepdims=True) + EPS)
            SEC[r, :] = (c * rs * GV[2:3, :] + GV[3:4, :]).astype(bf16)
            STATS[r, 2:3] = mean
            STATS[r, 3:4] = rs

        loop(TILE // unit, norm)

    loop(tiles, p3)

    cp_up.wait()
    cp_dn.wait()
    og_local().wait()
    S2, S2S, S2R, STS, STR = (s[n] for n in ("S2", "S2S", "S2R", "STS", "STR"))
    k_s2, k_st = rt.take(tiles), rt.take(tiles)

    def s2_remote(m):
        rows = ds(m * TILE, TILE)
        return rt.remote(S2S.at[rows, :], S2R.at[rows, :], rt.beside, sem=k_s2 + m)

    def st_remote(m):
        return rt.remote(STS.at[m], STR.at[m], rt.beside, sem=k_st + m)

    def row_sums(m, own, send, out, gain, src, k):
        unit = 32

        def split_rows(i):
            r = ds(m * TILE + i * unit, unit)
            b = ds(i * unit, unit)
            own[r, :] = PB[b, mine]
            send[r, :] = PB[b, away].astype(bf16)
            e = PB[b, :] * GV[gain : gain + 1, :]
            nh = (src[r, :].astype(f32) - STATS[r, k : k + 1]) * STATS[r, k + 1 : k + 2]
            SCOL[b, 0:1] = jnp.sum(e, axis=1, keepdims=True)
            SCOL[b, 1:2] = jnp.sum(e * nh, axis=1, keepdims=True)

        loop(TILE // unit, split_rows)
        out[m] = jnp.transpose(SCOL[...])[0:8, :]

    SCOL[...] = jnp.zeros_like(SCOL)

    def p4(m):
        og_remote(m).wait()
        rows = ds(m * TILE, TILE)

        def chunk(n):
            cols = ds(n * CHUNK, CHUNK)
            HB[...] = nn(SEC[rows, :], UP[:, cols])
            AB[...] = nt(OG[rows, :], DN[cols, :])
            unit = 16

            def gelu(i):
                b = ds(i * unit, unit)
                r = ds(m * TILE + i * unit, unit)
                v = HB[b, :]
                v2 = v * v
                t = jnp.tanh(v * (C0 + C1 * v2))
                hf = 0.5 * t + 0.5
                act = v * hf
                slope = hf + act * (1.0 - hf) * (2 * C0 + 6 * C1 * v2)
                ACT[r, cols] = act.astype(bf16)
                HG[r, cols] = (AB[b, :] * slope).astype(bf16)

            loop(TILE // unit, gelu)

        loop(FL // CHUNK, chunk)
        PB[...] = nt(HG[rows, :], UP[...])
        row_sums(m, S2, S2S, STS, 2, RES, 2)
        s2_remote(m).start()
        st_remote(m).start()

    loop(tiles, p4)

    def total(name, rows, cols, order, acc, base=0, sends=None):
        steps = plan(rows, order)
        count = len(steps)
        if sends is None:
            sends = [s[f"{name}S{k}"] for k in range(count)]
        recvs = [s[f"{name}R{k}"] for k in range(count)]
        return Total(rt, rows, cols, order, acc, base, sends, recvs, s[f"{name}O"])

    dg = total("D", FL, D, orders[0], s["DA"])
    ug_sends = [dg.sends[0]] + [s[f"US{k}"] for k in range(1, len(plan(FL, orders[1])))]
    ug = total("U", FL, D, orders[1], s["UA"], sends=ug_sends)

    def grad_half(left, right, first, rows, tall, store):
        def one(j):
            cols = ds(first + j * tall, tall, 128)
            store(ds(j * tall, tall), tn(left[:, cols], right))

        loop(rows // tall, one)

    def to_low(ref):
        def store(r, v):
            ref[r, :] = v.astype(bf16)

        return store

    def to_full(ref):
        def store(r, v):
            ref[r, :] = v

        return store

    grad_half(ACT, OG[...], (1 - core) * (FL // 2), FL // 2, 384, to_low(dg.sends[0]))
    dg.first_sent()
    grad_half(ACT, OG[...], core * (FL // 2), FL // 2, 384, to_full(dg.acc))
    dg.move()
    hg_half = lambda c: HG[:, ds(c * (FL // 2), FL // 2, 128)]
    grad_half(SEC, hg_half(1 - core), 0, D, 384, to_low(ug.sends[0]))
    ug.first_sent()
    grad_half(SEC, hg_half(core), 0, D, 384, to_full(ug.acc))
    ug.move()

    BG, GACC, MG = HG.at[:, pl.ds(3 * DL, DL)], s["GACC"], SEC
    GACC[...] = jnp.zeros_like(GACC)

    def norm_back(m, own, recv, sums, got, gain, src, k, base, write, slot):
        unit = 16
        SCOL[...] = jnp.transpose(
            jnp.concatenate([sums[m] + got[m], jnp.zeros((120, TILE), f32)], axis=0)
        ) * (1.0 / D)

        def rowsback(i):
            r = ds(m * TILE + i * unit, unit)
            b = ds(i * unit, unit)
            e = own[r, :] + recv[r, :].astype(f32)
            nh = (src[r, mine].astype(f32) - STATS[r, k : k + 1]) * STATS[r, k + 1 : k + 2]
            grad = STATS[r, k + 1 : k + 2] * (
                e * GV[gain : gain + 1, mine] - SCOL[b, 0:1] - nh * SCOL[b, 1:2]
            )
            write(r, base(r) + grad)
            en = e * nh
            GACC[slot] += en[0:8] + en[8:16]
            GACC[slot + 1] += e[0:8] + e[8:16]

        loop(TILE // unit, rowsback)

    def p5(m):
        s2_remote(m).wait()
        st_remote(m).wait()

        def write(r, v):
            S2[r, :] = v
            BG[r, :] = v.astype(bf16)

        norm_back(m, S2, S2R, STS, STR, 2, RES, 2, lambda r: OG[r, mine].astype(f32), write, 2)
        rows = ds(m * TILE, TILE)
        MG[rows, :] = nt(BG[rows, :], OW[:, mine]).astype(bf16)

    loop(tiles, p5)

    CGS, CGR, CGO = s["CGS"], s["CGR"], s["CGO"]

    def reduce_pair(h, p):
        members(h, p)
        lanes = ds((h * NP + p) * 128, 128)
        return fold(nn(MB[...], MG[:, lanes]))

    for p in range(NP):
        CGS[p] = reduce_pair(1 - hd, p)
    cp_cg = rt.remote(CGS, CGR, rt.beside)
    cp_cg.start()

    MA, MXS, MXR = s["MA"], MIX.at[pl.ds(0, DL), away], s["MXR"]
    MXS[...] = tn(MIX[:, away], BG[...]).astype(bf16)
    cp_mx = rt.remote(MXS, MXR, rt.beside)
    cp_mx.start()
    for p in range(NP):
        CGO[p] = reduce_pair(hd, p)
    MA[ds(hd * DL, DL, 16), :] = tn(MIX[:, mine], BG[...])

    dg.move()

    FFS, FFR = MIX.at[:, mine], s["FFR"]
    k_ff = rt.take(tiles)

    def ff_remote(m):
        rows = ds(m * TILE, TILE)
        return rt.remote(FFS.at[rows, :], FFR.at[rows, :], rt.beside, sem=k_ff + m)

    def p6(m):
        rows = ds(m * TILE, TILE)
        PB[...] = nn(ACT[rows, :], DN[...])
        unit = 32

        def split_rows(i):
            r = ds(m * TILE + i * unit, unit)
            b = ds(i * unit, unit)
            RES[r, mine] += PB[b, mine]
            FFS[r, :] = PB[b, away].astype(bf16)

        loop(TILE // unit, split_rows)
        ff_remote(m).start()

    loop(tiles, p6)
    ug.move()

    PG = HG
    cp_cg.wait()
    for p in range(NP):
        lanes = pl.ds(p * 128, 128)
        cog = split((CGO[p] + CGR[p]).astype(bf16))
        SB[...] = nt(CEN[p], QKV[1, :, lanes])
        DB[...] = nt(cog, QKV[2, :, lanes])
        unit = 16

        def back(i):
            r = ds(i * unit, unit)
            pr = jnp.exp(masked_scores(p, r) - AUX[p, r, 2:3])
            WB[r, :] = pr.astype(bf16)
            dp = DB[r, :]
            dot = jnp.sum(dp * pr, axis=1, keepdims=True)
            MB[r, :] = (pr * (dp - dot)).astype(bf16)

        loop(2 * CPAD // unit, back)
        cg = (nn(MB[...], QKV[1, :, lanes]) * (SCALE * AUX[p, :, 0:1])).astype(bf16)
        cg = split(fold(cg))
        for m in range(tiles):
            rows = pl.ds(m * TILE, TILE)
            at = p * 128
            PG[rows, at : at + 128] = nn(columns(own_ids(rows), p), cg).astype(bf16)
            PG[rows, DL + at : DL + at + 128] = (tn(MB[:, rows], CEN[p]) * SCALE).astype(bf16)
            PG[rows, 2 * DL + at : 2 * DL + at + 128] = tn(WB[:, rows], cog).astype(bf16)

    F1, F1S, F1R = RES.at[:, away], S2S, s["F1R"]
    FTS, FTR = s["FTS"], s["FTR"]
    k_f1, k_ft = rt.take(tiles), rt.take(tiles)

    def f1_remote(m):
        rows = ds(m * TILE, TILE)
        return rt.remote(F1S.at[rows, :], F1R.at[rows, :], rt.beside, sem=k_f1 + m)

    def ft_remote(m):
        return rt.remote(FTS.at[m], FTR.at[m], rt.beside, sem=k_ft + m)

    def p8(m):
        rows = ds(m * TILE, TILE)
        acc = nt(PG[rows, 0:DL], W[0])
        acc += nt(PG[rows, DL : 2 * DL], W[1])
        acc += nt(PG[rows, 2 * DL : 3 * DL], W[2])
        PB[...] = acc
        row_sums(m, F1, F1S, FTS, 0, X, 0)
        f1_remote(m).start()
        ft_remote(m).start()

    loop(tiles, p8)
    dg.move()

    def act_sends(rows, order, block):
        sends, at = [], 0
        for step, count, halve in plan(rows, order):
            sends.append(ACT.at[pl.ds(at, count), pl.ds(block * DL, DL)])
            at += count
        return sends

    grads = []
    for i in (2, 1, 0):
        name = "QKV"[i]
        tot = total(name, D, DL, orders[2 + i], s[f"{name}A"], 0, act_sends(D, orders[2 + i], i))
        right = PG[:, i * DL : (i + 1) * DL]
        grad_half(NRM, right, (1 - core) * (D // 2), D // 2, 384, to_low(tot.sends[0]))
        tot.first_sent()
        grad_half(NRM, right, core * (D // 2), D // 2, 384, to_full(tot.acc))
        grads.append(tot)
    vg, kg, qg = grads
    cp_mx.wait()
    mg = total("M", D, DL, orders[5], MA, core * DL, act_sends(D, orders[5], 3))

    def spread(i):
        MA[ds((1 - hd) * DL + i * 16, 16), :] = MXR[ds(i * 16, 16), :].astype(f32)

    loop(DL // 16, spread)

    def mix_half(i):
        mg.sends[0][ds(i * 16, 16), :] = MA[ds((1 - core) * DL + i * 16, 16), :].astype(bf16)

    loop(DL // 16, mix_half)
    mg.first_sent()
    for tot in (vg, kg, qg, mg):
        tot.move()
    ug.move()
    dg.move()

    LO, IG = S2R, BG

    def p9(m):
        ff_remote(m).wait()
        unit = 32

        def rows_out(i):
            r = ds(m * TILE + i * unit, unit)
            LO[r, :] = (RES[r, mine] + FFR[r, :].astype(f32)).astype(bf16)

        loop(TILE // unit, rows_out)

    loop(tiles, p9)
    cp_lo = rt.local(LO, lo_out)
    cp_lo.start()
    for tot in (ug, dg, vg, kg, qg, mg):
        tot.move()

    def p10(m):
        f1_remote(m).wait()
        ft_remote(m).wait()

        def write(r, v):
            IG[r, :] = v.astype(bf16)

        norm_back(m, F1, F1R, FTS, FTR, 0, X, 0, lambda r: S2[r, :], write, 0)

    loop(tiles, p10)
    cp_ig = rt.local(IG, ig_out)
    cp_ig.start()

    GX, GR, GO = s["GX"], s["GR"], s["GO"]
    for k in range(4):
        GX[0, k : k + 1, :] = jnp.sum(GACC[k], axis=0, keepdims=True)
    GX[0, 4:8, :] = jnp.zeros((4, DL), f32)
    done = [cp_lo, cp_ig]

    def finish(tot, src, dst):
        copy = rt.local(src, dst)
        copy.start()
        done.append(copy)

    totals = [
        (dg, lambda: finish(dg, s["DO"], d_out)),
        (ug, lambda: [finish(ug, s["UO"].at[pl.ds(j * D, D), :], u_out.at[:, pl.ds(j * D, D)]) for j in range(2)]),
        (vg, lambda: finish(vg, s["VO"], q_out.at[2])),
        (kg, lambda: finish(kg, s["KO"], q_out.at[1])),
        (qg, lambda: finish(qg, s["QO"], q_out.at[0])),
        (mg, lambda: [finish(mg, s["MO"].at[pl.ds(j * DL, DL), :], m_out.at[:, pl.ds(j * DL, DL)]) for j in range(2)]),
    ]
    gain_copy = None
    gain_step = 0

    def gain_move():
        nonlocal gain_copy, gain_step
        if gain_step > nbits + 1:
            return
        if gain_copy is not None:
            gain_copy.wait()
            if gain_step <= nbits:
                GX[gain_step] = GX[gain_step - 1] + GR[gain_step - 1]
            else:
                GO[:, away] = GR[nbits]
                GO[:, mine] = GX[nbits]
                copy = rt.local(GO, g_out)
                copy.start()
                done.append(copy)
        if gain_step < nbits:
            gain_copy = rt.remote(GX.at[gain_step], GR.at[gain_step], rt.across(1 << gain_step))
            gain_copy.start()
        elif gain_step == nbits:
            gain_copy = rt.remote(GX.at[nbits], GR.at[nbits], rt.beside)
            gain_copy.start()
        gain_step += 1

    gain_move()
    while any(tot.left for tot, _ in totals):
        for tot, end in totals:
            if tot.left:
                tot.move()
                if not tot.left:
                    end()
        gain_move()
    while gain_step <= nbits + 1:
        gain_move()
    for copy in done:
        copy.wait()


def layer(nbits, args):
    x, og, w, ow, up, dn, ids, gv = args
    T, DL = x.shape
    D, FL = up.shape
    NP = DL // 128
    bits = [1 << k for k in range(nbits)]
    order_a = list(bits)
    order_b = [bits[0]] + ([bits[2], bits[1]] + bits[3:] if nbits > 2 else bits[1:])
    orders = [order_a, order_b, order_a, order_b, order_a, order_b]
    tiles = T // TILE
    V = pltpu.VMEM
    scratch = [
        ("X", V((T, D), bf16)),
        ("OG", V((T, D), bf16)),
        ("NRM", V((T, D), bf16)),
        ("QKV", V((3, T, DL), bf16)),
        ("W", V((3, D, DL), bf16)),
        ("OW", V((D, D), bf16)),
        ("UP", V((D, FL), bf16)),
        ("DN", V((FL, D), bf16)),
        ("IDS", V((2, 8, T), i32)),
        ("IDE", V((2, 8, T), i32)),
        ("IDT", V((T, 16), i32)),
        ("GV", V((4, D), f32)),
        ("STATS", V((T, 8), f32)),
        ("AUX", V((NP, 2 * CPAD, 8), f32)),
        ("MIX", V((T, D), bf16)),
        ("RES", V((T, D), f32)),
        ("SEC", V((T, D), bf16)),
        ("ACT", V((T, FL), bf16)),
        ("HG", V((T, FL), bf16)),
        ("MB", V((2 * CPAD, T), bf16)),
        ("SB", V((2 * CPAD, T), f32)),
        ("DB", V((2 * CPAD, T), f32)),
        ("WB", V((2 * CPAD, T), bf16)),
        ("CEN", V((NP, 2 * CPAD, 128), bf16)),
        ("CO", V((2 * NP, CPAD, 128), bf16)),
        ("SCOL", V((TILE, 128), f32)),
        ("S2", V((T, DL), f32)),
        ("S2S", V((T, DL), bf16)),
        ("S2R", V((T, DL), bf16)),
        ("STS", V((tiles, 8, TILE), f32)),
        ("STR", V((tiles, 8, TILE), f32)),
        ("GACC", V((4, 8, DL), f32)),
        ("CGS", V((NP, CPAD, 128), f32)),
        ("CGR", V((NP, CPAD, 128), f32)),
        ("CGO", V((NP, CPAD, 128), f32)),
        ("MA", V((D, DL), f32)),
        ("MXR", V((DL, DL), bf16)),
        ("FFR", V((T, DL), bf16)),
        ("F1R", V((T, DL), bf16)),
        ("FTS", V((tiles, 8, TILE), f32)),
        ("FTR", V((tiles, 8, TILE), f32)),
        ("GX", V((nbits + 1, 8, DL), f32)),
        ("GR", V((nbits + 1, 8, DL), f32)),
        ("GO", V((8, D), f32)),
        ("DA", V((FL // 2, D), f32)),
        ("UA", V((D, FL // 2), f32)),
        ("QA", V((D // 2, DL), f32)),
        ("KA", V((D // 2, DL), f32)),
        ("VA", V((D // 2, DL), f32)),
    ]
    for name, rows, cols, order, own in (
        ("D", FL, D, orders[0], True),
        ("U", FL, D, orders[1], True),
        ("Q", D, DL, orders[2], False),
        ("K", D, DL, orders[3], False),
        ("V", D, DL, orders[4], False),
        ("M", D, DL, orders[5], False),
    ):
        for k, (step, count, halve) in enumerate(plan(rows, order)):
            if own and (name, k) != ("U", 0):
                scratch.append((f"{name}S{k}", V((count, cols), bf16)))
            scratch.append((f"{name}R{k}", V((count, cols), bf16)))
        scratch.append((f"{name}O", V((rows, cols), bf16)))
    copies = 6 * tiles + 16 + NP + 12 * nbits + nbits
    scratch += [
        ("send_sem", pltpu.SemaphoreType.DMA((copies,))),
        ("recv_sem", pltpu.SemaphoreType.DMA((copies,))),
        ("local_sem", pltpu.SemaphoreType.DMA((tiles + 24,))),
    ]
    shape = jax.ShapeDtypeStruct
    hbm = pl.BlockSpec(memory_space=pl.ANY)
    return pl.pallas_call(
        functools.partial(layer_kernel, [n for n, _ in scratch], nbits, orders),
        out_shape=(
            shape((T, DL), bf16),
            shape((T, DL), bf16),
            shape((3, D, DL), bf16),
            shape((DL, D), bf16),
            shape((D, FL), bf16),
            shape((FL, D), bf16),
            shape((8, D), f32),
        ),
        in_specs=[hbm] * 8,
        out_specs=(hbm,) * 7,
        scratch_shapes=[v for _, v in scratch],
        compiler_params=pltpu.CompilerParams(
            collective_id=0, has_side_effects=True, vmem_limit_bytes=67043328
        ),
        name="layer",
    )(x, og, w, ow, up, dn, ids, gv)


def shards(
    nbits,
    layer_input,
    first_gain,
    first_shift,
    qkv_weight,
    out_weight,
    second_gain,
    second_shift,
    up_weight,
    down_weight,
    segment_ids,
    pad_mask,
    cluster_ids,
    output_grad,
):
    ids = jnp.concatenate([cluster_ids, segment_ids[None], pad_mask[None]], axis=0)
    gains = jnp.stack([first_gain, first_shift, second_gain, second_shift])
    lo, ig, q, m, u, d, g = layer(
        nbits,
        (layer_input, output_grad, qkv_weight, out_weight, up_weight, down_weight, ids, gains),
    )
    return (lo, ig, q.astype(f32), m.astype(f32), u.astype(f32), d.astype(f32), g[0], g[1], g[2], g[3])


def solution(mesh):
    nbits = mesh.shape["dp"].bit_length() - 1
    placed = (
        P("dp", "head"),
        P(),
        P(),
        P(None, None, "head"),
        P("head", None),
        P(),
        P(),
        P(None, "head"),
        P("head", None),
        P("dp"),
        P("dp"),
        P("head", "dp"),
        P("dp", "head"),
    )
    return jax.shard_map(
        functools.partial(shards, nbits),
        mesh=mesh,
        in_specs=placed,
        out_specs=(
            P("dp", "head"),
            P("dp", "head"),
            P(None, None, "head"),
            P("head", None),
            P(None, "head"),
            P("head", None),
            P(),
            P(),
            P(),
            P(),
        ),
        check_vma=False,
    )
```

time: 623 us -> 239 us (0.38); the launches traced: 614 us -> 239 us
  waiting for transfers between devices: 389 us -> 0 us
  Pallas kernels: 0 us -> 220 us
  matrix products: 85.2 us -> 0 us
  blocking collectives: 64.1 us -> 0 us
  local copies, waits for them, and re-layouts: 34.1 us -> 6.1 us
  between operations: 15 us -> 0.66 us
  other arithmetic: 26.2 us -> 12.3 us
    psum x3 -> x0, waiting for transfers between devices: 291 us -> none  [the longest x1 190 us: shards(): lax.psum((qkv_grad, mix_weight_grad, up_grad, down_grad, first_gain_grad,...]
    pallas_call x0 -> x1, Pallas kernels: none -> 220 us  [layer(): pl.pallas_call(functools.partial(layer_kernel, [n for n, _ in scratch], n...]
    dot_general x22 -> x0, matrix products: 85.2 us -> none  [the longest x1 9.72 us: shards(): hidden = jnp.dot(second, up_weight, preferred_element_type=jnp.float32)]
    all_gather x3 -> x0, waiting for transfers between devices: 71.5 us -> none  [the longest x1 25.7 us: shards(): lax.all_gather(layer_input, 'head', axis=1, tiled=True).astype(jnp.float32)]
    psum x1 -> x0, blocking collectives: 64.1 us -> none  [shards(): lax.psum((qkv_grad, mix_weight_grad, up_grad, down_grad, first_gain_grad,...]
    unnamed x74 -> x12, local copies, waits for them, and re-layouts: 29.2 us -> 1.78 us
    unnamed x10 -> x0, waiting for transfers between devices: 27 us -> none
    reduce_sum x8 -> x0, other arithmetic: 14.6 us -> none  [the longest x1 4.56 us: shards(): first_gain_grad = jnp.sum(first_back * first_hat, axis=0)]
  transfers between devices with their start and end apart: 8 -> 0, of which waited for: 7 -> 0; matrix products, arithmetic and copies ran while one was open for 15% -> 0% of each run, Pallas kernels for 0% -> 0%
where the time goes in v1:
time: 239 us
  Pallas kernels  220 us (92%)
  other arithmetic  12.3 us (5%)
  local copies, waits for them, and re-layouts  6.1 us (3%)
    pallas_call x1, Pallas kernels, layer(): pl.pallas_call(functools.partial(layer_kernel, [n for n, _ in scratch], n...  220 us

profile of v1, /device:TPU:0, one launch (start us, length us, event | category | flops | bytes accessed | tf_op | source)
XLA Modules:
  0.0 238.7 jit_solution(11496670846843139015)
XLA Ops:
  0.6 1.4 pad_add_fusion.refs_6_
  2.1 0.7 stack.15
  2.8 0.7 stack.16
  3.4 0.7 stack.17
  4.1 0.7 stack.18
  4.8 0.6 pad_maximum_fusion.refs_7_
  5.4 219.6 %layer.1 = (bf16[1024,384]{1,0:T(8,128)(2,1)}, bf16[1024,384]{1,0:T(8,128)(2,1)}, bf16[3,768,384]{2,1,0:T(8,128)(2,1)}, bf16[384,768]{1,0:T(8,128)(2,1)}, bf16[7...) custom-call(bf16[1024,384]{1,0:T(8,128)(2,1)} %refs_0_.1, bf16[1024,384]{1,0:T(8,128)(2,1)} %refs_1_.1, ...), custom_call_target="tpu_custom_call" | custom-call | tf_op jit(solution)/shard_map/layer/pallas_call | solution.py:875
  225.0 1.6 slice_reduce_fusion
  226.6 0.0 copy-start
  226.6 4.6 %convert_element_type.14 = f32[768,1536]{1,0:T(8,128)} convert(bf16[768,1536]{1,0:T(8,128)(2,1)} %get-tuple-element.21) | non-fusion elementwise | flops 1179648 | bytes 7077888 | tf_op jit(solution)/shard_map/convert_element_type | solution.py:918
  231.2 0.0 copy-done
  231.2 0.0 copy-start.1
  231.2 2.5 %convert_element_type.15 = f32[1536,768]{1,0:T(8,128)} convert(bf16[1536,768]{1,0:T(8,128)(2,1)S(1)} %copy-done) | non-fusion elementwise | flops 1179648 | bytes 7077888 | tf_op jit(solution)/shard_map/convert_element_type | solution.py:918
  233.8 0.0 copy-done.1
  233.8 0.0 copy-start.4
  233.8 0.0 copy-start.3
  233.8 2.0 convert_element_type.12
  235.8 0.0 copy-start.2
  235.8 0.0 copy-done.4
  235.8 1.1 convert_element_type.13
  236.9 0.0 copy-done.3
  236.9 0.9 copy.25
  237.8 0.0 copy-done.2
  237.8 0.9 copy.26
Async XLA Ops:
  226.6 4.7 %copy-start = (bf16[1536,768]{1,0:T(8,128)(2,1)S(1)}, bf16[1536,768]{1,0:T(8,128)(2,1)}, u32[]{:S(2)}) copy-start(bf16[1536,768]{1,0:T(8,128)(2,1)} %get-tuple-element.22) | copy-start | bytes 7077892
  231.2 2.5 %copy-start.1 = (bf16[3,768,384]{2,1,0:T(8,128)(2,1)S(1)}, bf16[3,768,384]{2,1,0:T(8,128)(2,1)}, u32[]{:S(2)}) copy-start(bf16[3,768,384]{2,1,0:T(8,128)(2,1)} %get-tuple-element.19) | copy-start | bytes 5308420
  233.8 2.0 copy-start.4
  233.8 3.1 %copy-start.3 = (bf16[1024,384]{1,0:T(8,128)(2,1)S(1)}, bf16[1024,384]{1,0:T(8,128)(2,1)}, u32[]{:S(2)}) copy-start(bf16[1024,384]{1,0:T(8,128)(2,1)} %get-tuple-element.38) | copy-start | bytes 2359300
  235.8 2.0 copy-start.2

commit v2 on v1

--- a/solution.py
+++ b/solution.py
@@ -12,6 +12,8 @@
 CPAD = 128
 TILE = 256
 CHUNK = 512
+UN, UA, UG = 8, 16, 16
+SCHED = {"r": "D", "f": "U", "b0": "D", "b1": "U", "b2": "D", "o": "U", "v": "D", "k": "VU", "q": "K", "m": "QDV", "l": "MUKQ", "e": "DVM"}
 EPS = 1e-05
 FAR = -1e30
 SCALE = HDIM**-0.5
@@ -39,12 +41,20 @@
     return pl.ds(pl.multiple_of(start, size if unit is None else unit), size)
 
 
-def loop(count, body):
+def loop(count, body, unroll=1):
+    while count % unroll:
+        unroll -= 1
+    if count == unroll:
+        for i in range(count):
+            body(i)
+        return
+
     def step(i, carry):
-        body(i)
+        for j in range(unroll):
+            body(i * unroll + j)
         return carry
 
-    lax.fori_loop(0, count, step, 0)
+    lax.fori_loop(0, count // unroll, step, 0)
 
 
 def plan(rows, order):
@@ -108,7 +118,7 @@
                         a = ds(base + away + i * unit, unit)
                         out[ds(i * unit, unit), :] = self.join(acc, a, recv, own, r).astype(bf16)
 
-                    loop(nrows // unit, cast)
+                    loop(nrows // unit, cast, 4)
                     self.send(k + 1)
 
                     def add(i):
@@ -116,7 +126,7 @@
                         a = ds(base + kept + i * unit, unit)
                         acc[a, :] = self.join(acc, a, recv, own, r)
 
-                    loop(nrows // unit, add)
+                    loop(nrows // unit, add, 4)
                     self.base = base + kept
                     self.at = self.at + kept
                     self.size = nrows
@@ -129,7 +139,7 @@
                         acc[a, :] = v
                         out[r, :] = v.astype(bf16)
 
-                    loop(nrows // unit, both)
+                    loop(nrows // unit, both, 4)
                     self.send(k + 1)
             else:
 
@@ -139,7 +149,7 @@
                     o = ds(self.at + i * unit, unit)
                     self.out[o, :] = self.join(acc, a, recv, own, r).astype(bf16)
 
-                loop(rows // unit, last)
+                loop(rows // unit, last, 4)
                 self.todo = [j for j in range(n) if self.steps[j][2]]
                 self.gather()
             return
@@ -281,8 +291,6 @@
         rt.beside,
     )
     cp_owr.start()
-    og_remote(0).start()
-    og_remote(1).start()
 
     cp_ids.wait()
     cp_idr.wait()
@@ -310,7 +318,7 @@
             STATS[r, 0:1] = mean
             STATS[r, 1:2] = rs
 
-        loop(TILE // unit, norm)
+        loop(TILE // unit, norm, UN)
         rows = ds(m * TILE, TILE)
         for i in range(3):
             QKV[i, rows, :] = nn(NRM[rows, :], W[i]).astype(bf16)
@@ -342,7 +350,7 @@
                 c = lax.broadcasted_iota(i32, (unit, T), 0) + i * unit
                 MB[ds(a * CPAD + i * unit, unit), :] = jnp.where(row == c, 1.0, 0.0).astype(bf16)
 
-            loop(CPAD // unit, fill)
+            loop(CPAD // unit, fill, UA)
 
     def columns(cols, p):
         lane = lax.broadcasted_iota(i32, (TILE, CPAD), 1)
@@ -374,7 +382,7 @@
             AUX[p, r, 0:1] = 1.0 / n
             AUX[p, r, 1:2] = jnp.sum(v * seg, axis=1, keepdims=True) / n
 
-        loop(2 * CPAD // unit, count)
+        loop(2 * CPAD // unit, count, UA)
         cen = (nn(MB[...], QKV[0, :, lanes]) * AUX[p, :, 0:1]).astype(bf16)
         CEN[p] = split(fold(cen))
         SB[...] = nt(CEN[p], QKV[1, :, lanes])
@@ -388,14 +396,14 @@
             WB[r, :] = (e * (1.0 / den)).astype(bf16)
             AUX[p, r, 2:3] = top + jnp.log(den)
 
-        loop(2 * CPAD // unit, soft)
+        loop(2 * CPAD // unit, soft, UA)
         CO[hd * NP + p] = fold(nn(WB[...], QKV[2, :, lanes]).astype(bf16))
         there = CO.at[hd * NP + p]
         copy = rt.remote(there, there, rt.beside)
         copy.start()
         co_sent.append(copy)
 
-    for m in range(2, tiles):
+    for m in range(tiles):
         og_remote(m).start()
 
     cp_ow.wait()
@@ -422,7 +430,7 @@
             STATS[r, 2:3] = mean
             STATS[r, 3:4] = rs
 
-        loop(TILE // unit, norm)
+        loop(TILE // unit, norm, UN)
 
     loop(tiles, p3)
 
@@ -452,7 +460,7 @@
             SCOL[b, 0:1] = jnp.sum(e, axis=1, keepdims=True)
             SCOL[b, 1:2] = jnp.sum(e * nh, axis=1, keepdims=True)
 
-        loop(TILE // unit, split_rows)
+        loop(TILE // unit, split_rows, UN)
         out[m] = jnp.transpose(SCOL[...])[0:8, :]
 
     SCOL[...] = jnp.zeros_like(SCOL)
@@ -479,7 +487,7 @@
                 ACT[r, cols] = act.astype(bf16)
                 HG[r, cols] = (AB[b, :] * slope).astype(bf16)
 
-            loop(TILE // unit, gelu)
+            loop(TILE // unit, gelu, UG)
 
         loop(FL // CHUNK, chunk)
         PB[...] = nt(HG[rows, :], UP[...])
@@ -529,6 +537,12 @@
     ug.first_sent()
     grad_half(SEC, hg_half(core), 0, D, 384, to_full(ug.acc))
     ug.move()
+
+    sums = {"D": dg, "U": ug}
+
+    def point(name):
+        for one in SCHED.get(name, ""):
+            sums[one].move()
 
     BG, GACC, MG = HG.at[:, pl.ds(3 * DL, DL)], s["GACC"], SEC
     GACC[...] = jnp.zeros_like(GACC)
@@ -552,7 +566,7 @@
             GACC[slot] += en[0:8] + en[8:16]
             GACC[slot + 1] += e[0:8] + e[8:16]
 
-        loop(TILE // unit, rowsback)
+        loop(TILE // unit, rowsback, UN)
 
     def p5(m):
         s2_remote(m).wait()
@@ -576,7 +590,7 @@
         return fold(nn(MB[...], MG[:, lanes]))
 
     for p in range(NP):
-        CGS[p] = reduce_pair(1 - hd, p)
+        CGS[p] = reduce_pair(1 - hd, p).astype(bf16)
     cp_cg = rt.remote(CGS, CGR, rt.beside)
     cp_cg.start()
 
@@ -588,7 +602,7 @@
         CGO[p] = reduce_pair(hd, p)
     MA[ds(hd * DL, DL, 16), :] = tn(MIX[:, mine], BG[...])
 
-    dg.move()
+    point("r")
 
     FFS, FFR = MIX.at[:, mine], s["FFR"]
     k_ff = rt.take(tiles)
@@ -608,17 +622,18 @@
             RES[r, mine] += PB[b, mine]
             FFS[r, :] = PB[b, away].astype(bf16)
 
-        loop(TILE // unit, split_rows)
+        loop(TILE // unit, split_rows, UN)
+
+    loop(tiles, p6)
+    for m in range(tiles // 2):
         ff_remote(m).start()
-
-    loop(tiles, p6)
-    ug.move()
+    point("f")
 
     PG = HG
     cp_cg.wait()
     for p in range(NP):
         lanes = pl.ds(p * 128, 128)
-        cog = split((CGO[p] + CGR[p]).astype(bf16))
+        cog = split((CGO[p] + CGR[p].astype(f32)).astype(bf16))
         SB[...] = nt(CEN[p], QKV[1, :, lanes])
         DB[...] = nt(cog, QKV[2, :, lanes])
         unit = 16
@@ -631,7 +646,7 @@
             dot = jnp.sum(dp * pr, axis=1, keepdims=True)
             MB[r, :] = (pr * (dp - dot)).astype(bf16)
 
-        loop(2 * CPAD // unit, back)
+        loop(2 * CPAD // unit, back, 8)
         cg = (nn(MB[...], QKV[1, :, lanes]) * (SCALE * AUX[p, :, 0:1])).astype(bf16)
         cg = split(fold(cg))
         for m in range(tiles):
@@ -640,6 +655,7 @@
             PG[rows, at : at + 128] = nn(columns(own_ids(rows), p), cg).astype(bf16)
             PG[rows, DL + at : DL + at + 128] = (tn(MB[:, rows], CEN[p]) * SCALE).astype(bf16)
             PG[rows, 2 * DL + at : 2 * DL + at + 128] = tn(WB[:, rows], cog).astype(bf16)
+        point(f"b{p}")
 
     F1, F1S, F1R = RES.at[:, away], S2S, s["F1R"]
     FTS, FTR = s["FTS"], s["FTR"]
@@ -663,7 +679,9 @@
         ft_remote(m).start()
 
     loop(tiles, p8)
-    dg.move()
+    for m in range(tiles // 2, tiles):
+        ff_remote(m).start()
+    point("o")
 
     def act_sends(rows, order, block):
         sends, at = [], 0
@@ -672,15 +690,20 @@
             at += count
         return sends
 
+    while dg.pos < len(dg.steps):
+        dg.move()
     grads = []
     for i in (2, 1, 0):
         name = "QKV"[i]
-        tot = total(name, D, DL, orders[2 + i], s[f"{name}A"], 0, act_sends(D, orders[2 + i], i))
+        room = s["DA"].at[pl.ds(i // 2 * (D // 2), D // 2), pl.ds(i % 2 * DL, DL)]
+        tot = total(name, D, DL, orders[2 + i], room, 0, act_sends(D, orders[2 + i], i))
         right = PG[:, i * DL : (i + 1) * DL]
         grad_half(NRM, right, (1 - core) * (D // 2), D // 2, 384, to_low(tot.sends[0]))
         tot.first_sent()
         grad_half(NRM, right, core * (D // 2), D // 2, 384, to_full(tot.acc))
         grads.append(tot)
+        sums[name] = tot
+        point("qkv"[i])
     vg, kg, qg = grads
     cp_mx.wait()
     mg = total("M", D, DL, orders[5], MA, core * DL, act_sends(D, orders[5], 3))
@@ -695,10 +718,8 @@
 
     loop(DL // 16, mix_half)
     mg.first_sent()
-    for tot in (vg, kg, qg, mg):
-        tot.move()
-    ug.move()
-    dg.move()
+    sums["M"] = mg
+    point("m")
 
     LO, IG = S2R, BG
 
@@ -710,13 +731,12 @@
             r = ds(m * TILE + i * unit, unit)
             LO[r, :] = (RES[r, mine] + FFR[r, :].astype(f32)).astype(bf16)
 
-        loop(TILE // unit, rows_out)
+        loop(TILE // unit, rows_out, UN)
 
     loop(tiles, p9)
     cp_lo = rt.local(LO, lo_out)
     cp_lo.start()
-    for tot in (ug, dg, vg, kg, qg, mg):
-        tot.move()
+    point("l")
 
     def p10(m):
         f1_remote(m).wait()
@@ -730,6 +750,7 @@
     loop(tiles, p10)
     cp_ig = rt.local(IG, ig_out)
     cp_ig.start()
+    point("e")
 
     GX, GR, GO = s["GX"], s["GR"], s["GO"]
     for k in range(4):
@@ -833,8 +854,8 @@
         ("STS", V((tiles, 8, TILE), f32)),
         ("STR", V((tiles, 8, TILE), f32)),
         ("GACC", V((4, 8, DL), f32)),
-        ("CGS", V((NP, CPAD, 128), f32)),
-        ("CGR", V((NP, CPAD, 128), f32)),
+        ("CGS", V((NP, CPAD, 128), bf16)),
+        ("CGR", V((NP, CPAD, 128), bf16)),
         ("CGO", V((NP, CPAD, 128), f32)),
         ("MA", V((D, DL), f32)),
         ("MXR", V((DL, DL), bf16)),
@@ -847,9 +868,6 @@
         ("GO", V((8, D), f32)),
         ("DA", V((FL // 2, D), f32)),
         ("UA", V((D, FL // 2), f32)),
-        ("QA", V((D // 2, DL), f32)),
-        ("KA", V((D // 2, DL), f32)),
-        ("VA", V((D // 2, DL), f32)),
     ]
     for name, rows, cols, order, own in (
         ("D", FL, D, orders[0], True),

time: 239 us -> 192 us (0.80)
  Pallas kernels: 220 us -> 173 us
    pallas_call x1, Pallas kernels: 220 us -> 173 us  [layer(): pl.pallas_call(functools.partial(layer_kernel, [n for n, _ in scratch], n...]
where the time goes in v2:
time: 192 us
  Pallas kernels  173 us (90%)
  other arithmetic  12.3 us (6%)
  local copies, waits for them, and re-layouts  6.1 us (3%)
    pallas_call x1, Pallas kernels, layer(): pl.pallas_call(functools.partial(layer_kernel, [n for n, _ in scratch], n...  173 us
    convert_element_type x1, other arithmetic, shards(): u.astype(f32)  4.65 us

profile of v2, /device:TPU:0, one launch (start us, length us, event | category | flops | bytes accessed | tf_op | source)
XLA Modules:
  0.0 191.8 jit_solution(2166359371986120899)
XLA Ops:
  0.6 1.4 pad_add_fusion.refs_6_
  2.1 0.7 stack.15
  2.8 0.7 stack.16
  3.4 0.7 stack.17
  4.1 0.7 stack.18
  4.8 0.6 pad_maximum_fusion.refs_7_
  5.4 172.7 %layer.1 = (bf16[1024,384]{1,0:T(8,128)(2,1)}, bf16[1024,384]{1,0:T(8,128)(2,1)}, bf16[3,768,384]{2,1,0:T(8,128)(2,1)}, bf16[384,768]{1,0:T(8,128)(2,1)}, bf16[7...) custom-call(bf16[1024,384]{1,0:T(8,128)(2,1)} %refs_0_.1, bf16[1024,384]{1,0:T(8,128)(2,1)} %refs_1_.1, ...), custom_call_target="tpu_custom_call" | custom-call | tf_op jit(solution)/shard_map/layer/pallas_call | solution.py:893
  178.2 1.6 slice_reduce_fusion
  179.7 0.0 copy-start
  179.7 4.6 %convert_element_type.14 = f32[768,1536]{1,0:T(8,128)} convert(bf16[768,1536]{1,0:T(8,128)(2,1)} %get-tuple-element.21) | non-fusion elementwise | flops 1179648 | bytes 7077888 | tf_op jit(solution)/shard_map/convert_element_type | solution.py:936
  184.4 0.0 copy-done
  184.4 0.0 copy-start.1
  184.4 2.5 %convert_element_type.15 = f32[1536,768]{1,0:T(8,128)} convert(bf16[1536,768]{1,0:T(8,128)(2,1)S(1)} %copy-done) | non-fusion elementwise | flops 1179648 | bytes 7077888 | tf_op jit(solution)/shard_map/convert_element_type | solution.py:936
  186.9 0.0 copy-done.1
  186.9 0.0 copy-start.4
  186.9 0.0 copy-start.3
  186.9 2.0 %convert_element_type.12 = f32[3,768,384]{2,1,0:T(8,128)} convert(bf16[3,768,384]{2,1,0:T(8,128)(2,1)S(1)} %copy-done.1) | non-fusion elementwise | flops 884736 | bytes 5308416 | tf_op jit(solution)/shard_map/convert_element_type | solution.py:936
  189.0 0.0 copy-start.2
  189.0 0.0 copy-done.4
  189.0 1.1 convert_element_type.13
  190.1 0.0 copy-done.3
  190.1 0.9 copy.25
  190.9 0.0 copy-done.2
  190.9 0.9 copy.26
Async XLA Ops:
  179.7 4.7 %copy-start = (bf16[1536,768]{1,0:T(8,128)(2,1)S(1)}, bf16[1536,768]{1,0:T(8,128)(2,1)}, u32[]{:S(2)}) copy-start(bf16[1536,768]{1,0:T(8,128)(2,1)} %get-tuple-element.22) | copy-start | bytes 7077892
  184.4 2.5 %copy-start.1 = (bf16[3,768,384]{2,1,0:T(8,128)(2,1)S(1)}, bf16[3,768,384]{2,1,0:T(8,128)(2,1)}, u32[]{:S(2)}) copy-start(bf16[3,768,384]{2,1,0:T(8,128)(2,1)} %get-tuple-element.19) | copy-start | bytes 5308420
  186.9 2.0 %copy-start.4 = (bf16[384,768]{1,0:T(8,128)(2,1)S(1)}, bf16[384,768]{1,0:T(8,128)(2,1)}, u32[]{:S(2)}) copy-start(bf16[384,768]{1,0:T(8,128)(2,1)} %get-tuple-element.20) | copy-start | bytes 1769476
  186.9 3.1 %copy-start.3 = (bf16[1024,384]{1,0:T(8,128)(2,1)S(1)}, bf16[1024,384]{1,0:T(8,128)(2,1)}, u32[]{:S(2)}) copy-start(bf16[1024,384]{1,0:T(8,128)(2,1)} %get-tuple-element.38) | copy-start | bytes 2359300
  189.0 2.0 %copy-start.2 = (bf16[1024,384]{1,0:T(8,128)(2,1)S(1)}, bf16[1024,384]{1,0:T(8,128)(2,1)}, u32[]{:S(2)}) copy-start(bf16[1024,384]{1,0:T(8,128)(2,1)} %get-tuple-element.39) | copy-start | bytes 2359300
